TPU v7x, 32 devices: a whole 2x2x4 slice. The times are simulated.
32 devices in a mesh: inter: 16 (over z, y, core), intra: 2 (over x).
Axes of the slice: x: 2, y: 2, z: 4, core: 2. Of those that a mesh axis runs over, the one named last changes fastest.
Arguments:
- hidden_in: bfloat16 [16, 256, 4096], P('inter', 'intra'), may hold values from -120 to 120, as said below
- norm_gain: bfloat16 [4096], P(('inter', 'intra')), may hold values from 0.5 to 2, as said below
- qkv_weight: bfloat16 [4096, 768], P(('inter', 'intra')), may hold values from -0.09375 to 0.09375
- attn_cotangent: bfloat16 [16, 256, 512], P('inter', 'intra'), may hold values from -6 to 6
Outputs:
- attn: bfloat16 [16, 256, 512], P('inter', 'intra')
- grad_in: bfloat16 [16, 256, 4096], P('inter', 'intra')
- weight_grad: float32 [4096, 768], P(('intra', 'inter'))
- gain_grad: float32 [4096], P(('intra', 'inter'))
Inputs may be any that keep to these rules, and one draw needn't show every extreme that they name: `hidden_in`: activations with spread row and feature scales. `norm_gain`: positive gains.
All inputs are finite; a program needn't handle non-finite values.
Results may differ from a plain program's by a relative error of at most 0.015.
Values may be sent and summed in bfloat16 or wider, within the bound.
A program may use at most 64 MiB of HBM per device.

v0:
```python
import jax
import jax.numpy as jnp
from jax import lax
from jax.sharding import PartitionSpec as P

HD = 128
HEADS = 4


eps_norm = 1e-05
rope_base = 500000.0


def rope_tables(positions, head_size):
    half_size = head_size // 2
    freqs = rope_base ** (-jnp.arange(half_size, dtype=jnp.float32) / half_size)
    angles = positions.astype(jnp.float32)[:, None] * freqs[None, :]
    return (jnp.cos(angles), jnp.sin(angles))


def rotate(values_in, cosine, sine):
    half_size = values_in.shape[-1] // 2
    first, second = (values_in[..., :half_size], values_in[..., half_size:])
    return jnp.concatenate(
        [first * cosine - second * sine, second * cosine + first * sine], axis=-1
    )


def unrotate(grad_out, cosine, sine):
    half_size = grad_out.shape[-1] // 2
    first, second = (grad_out[..., :half_size], grad_out[..., half_size:])
    return jnp.concatenate(
        [first * cosine + second * sine, second * cosine - first * sine], axis=-1
    )


def forward_fold(query_rows, row_pos):

    def forward_advance(carry, piece, start):
        row_top, row_total, weighted = carry
        key_part, value_part = piece
        scores = jnp.einsum("qd,kd->qk", query_rows, key_part, preferred_element_type=jnp.float32)
        key_pos = jnp.arange(key_part.shape[0], dtype=jnp.int32)
        allowed = key_pos[None, :] <= row_pos[:, None]
        scores = jnp.where(allowed, scores, -1e30)
        new_top = jnp.maximum(row_top, jnp.max(scores, axis=1))
        numbers = jnp.where(allowed, jnp.exp(scores - new_top[:, None]), 0.0)
        row_total = jnp.sum(numbers, axis=1)
        weighted = jnp.dot(
            numbers,
            value_part.astype(jnp.float32),
            precision=lax.Precision.HIGHEST,
            preferred_element_type=jnp.float32,
        )
        return (new_top, row_total, weighted)

    return forward_advance


def query_grad_fold(query_rows, row_pos, grad_flat, log_total, row_delta):

    def query_advance(grad_query, piece, start):
        key_part, value_part = piece
        scores = jnp.einsum("qd,kd->qk", query_rows, key_part, preferred_element_type=jnp.float32)
        key_pos = jnp.arange(key_part.shape[0], dtype=jnp.int32)
        allowed = key_pos[None, :] <= row_pos[:, None]
        probs = jnp.where(
            allowed, jnp.exp(jnp.where(allowed, scores, -1e30) - log_total[:, None]), 0.0
        )
        grad_probs = jnp.einsum(
            "qd,kd->qk", grad_flat, value_part, preferred_element_type=jnp.float32
        )
        grad_scores = (probs * (grad_probs - row_delta[:, None])).astype(jnp.bfloat16)
        return jnp.dot(grad_scores, key_part, preferred_element_type=jnp.float32)

    return query_advance


def key_grad_fold(key_rows, value_rows, key_pos, log_all, delta_all, heads_count):

    def key_advance(carry, piece, start):
        query_part, attn_grad_part = piece
        count = query_part.shape[0]
        scores = jnp.einsum("qd,kd->qk", query_part, key_rows, preferred_element_type=jnp.float32)
        query_pos = jnp.arange(count, dtype=jnp.int32) // heads_count
        allowed = key_pos[None, :] <= query_pos[:, None]
        probs = jnp.where(
            allowed, jnp.exp(jnp.where(allowed, scores, -1e30) - log_all[:, None]), 0.0
        )
        grad_values = jnp.einsum(
            "qk,qd->kd",
            probs.astype(jnp.bfloat16),
            attn_grad_part,
            preferred_element_type=jnp.float32,
        )
        grad_probs = jnp.einsum(
            "qd,kd->qk", attn_grad_part, value_rows, preferred_element_type=jnp.float32
        )
        grad_scores = (probs * (grad_probs - delta_all[:, None])).astype(jnp.bfloat16)
        grad_keys = jnp.einsum(
            "qk,qd->kd", grad_scores, query_part, preferred_element_type=jnp.float32
        )
        return (grad_keys, grad_values)

    return key_advance


def local(hidden_in, norm_gain, qkv_weight, attn_cotangent):
    rows_in = hidden_in[0]
    grad_attn = attn_cotangent[0]
    tokens_here = rows_in.shape[0]
    width = rows_in.shape[1]
    head_size = HD
    heads_count = HEADS
    qcols = heads_count * head_size
    scale = head_size ** (-0.5)
    weight_group, gain_group = (
        lax.all_gather(qkv_weight, "intra", axis=0, tiled=True),
        lax.all_gather(norm_gain, "intra", axis=0, tiled=True),
    )
    weight_full, gain_full = (
        lax.all_gather(weight_group, "inter", axis=0, tiled=True),
        lax.all_gather(gain_group, "inter", axis=0, tiled=True),
    )
    query_pos = lax.axis_index("intra") * tokens_here + jnp.arange(tokens_here, dtype=jnp.int32)
    row_pos = jnp.broadcast_to(query_pos[:, None], (tokens_here, heads_count)).reshape(
        tokens_here * heads_count
    )
    cosine, sine = rope_tables(query_pos, head_size)
    wide_rows = rows_in.astype(jnp.float32)
    inv_rms = lax.rsqrt(jnp.mean(wide_rows * wide_rows, axis=1, keepdims=True) + eps_norm)
    normed = (wide_rows * inv_rms * gain_full.astype(jnp.float32)[None, :]).astype(jnp.bfloat16)
    mixed = jnp.dot(normed, weight_full, preferred_element_type=jnp.float32)
    query_rows = (
        (
            rotate(
                mixed[:, :qcols].reshape(tokens_here, heads_count, head_size),
                cosine[:, None, :],
                sine[:, None, :],
            )
            * scale
        )
        .astype(jnp.bfloat16)
        .reshape(tokens_here * heads_count, head_size)
    )
    key_rows = rotate(mixed[:, qcols : qcols + head_size], cosine, sine).astype(jnp.bfloat16)
    value_rows = mixed[:, qcols + head_size :].astype(jnp.bfloat16)
    grad_flat = grad_attn.reshape(tokens_here * heads_count, head_size)
    flat_rows = tokens_here * heads_count
    forward_step = forward_fold(query_rows, row_pos)
    start_carry = (
        jnp.full((flat_rows,), -1e30, jnp.float32),
        jnp.zeros((flat_rows,), jnp.float32),
        jnp.zeros((flat_rows, head_size), jnp.float32),
    )
    row_top, row_total, weighted = forward_step(
        start_carry,
        (
            lax.all_gather(key_rows, "intra", axis=0, tiled=True),
            lax.all_gather(value_rows, "intra", axis=0, tiled=True),
        ),
        jnp.int32(0),
    )
    attn_flat = (weighted / row_total[:, None]).astype(jnp.bfloat16)
    log_total = row_top + jnp.log(row_total)
    row_delta = jnp.sum(grad_flat.astype(jnp.float32) * attn_flat.astype(jnp.float32), axis=1)
    query_step = query_grad_fold(query_rows, row_pos, grad_flat, log_total, row_delta)
    grad_query = query_step(
        jnp.zeros((flat_rows, head_size), jnp.float32),
        (
            lax.all_gather(key_rows, "intra", axis=0, tiled=True),
            lax.all_gather(value_rows, "intra", axis=0, tiled=True),
        ),
        jnp.int32(0),
    )
    log_all, delta_all = (
        lax.all_gather(log_total, "intra", axis=0, tiled=True),
        lax.all_gather(row_delta, "intra", axis=0, tiled=True),
    )
    key_step = key_grad_fold(key_rows, value_rows, query_pos, log_all, delta_all, heads_count)
    grad_keys, grad_values = key_step(
        (
            jnp.zeros((tokens_here, head_size), jnp.float32),
            jnp.zeros((tokens_here, head_size), jnp.float32),
        ),
        (
            lax.all_gather(query_rows, "intra", axis=0, tiled=True),
            lax.all_gather(grad_flat, "intra", axis=0, tiled=True),
        ),
        jnp.int32(0),
    )
    query_back = (
        unrotate(
            grad_query.reshape(tokens_here, heads_count, head_size),
            cosine[:, None, :],
            sine[:, None, :],
        )
        * scale
    ).reshape(tokens_here, qcols)
    grad_mixed = jnp.concatenate(
        [query_back, unrotate(grad_keys, cosine, sine), grad_values], axis=1
    ).astype(jnp.bfloat16)
    weight_back, gain_back = (weight_full, gain_full)
    gain_wide = gain_back.astype(jnp.float32)[None, :]
    grad_normed = jnp.einsum(
        "tc,dc->td", grad_mixed, weight_back, preferred_element_type=jnp.float32
    )
    inner = jnp.sum(grad_normed * gain_wide * wide_rows, axis=1, keepdims=True)
    grad_rows = (
        gain_wide * grad_normed * inv_rms - wide_rows * inv_rms**3 / width * inner
    ).astype(jnp.bfloat16)
    gain_term = jnp.sum(grad_normed * wide_rows * inv_rms, axis=0)
    normed_cols = lax.all_to_all(normed, "intra", split_axis=1, concat_axis=0, tiled=True)
    group_term = lax.dot_general(
        normed_cols,
        lax.all_gather(grad_mixed, "intra", axis=0, tiled=True),
        (((0,), (0,)), ((), ())),
        preferred_element_type=jnp.float32,
    )
    term_low = lax.optimization_barrier(group_term.astype(jnp.bfloat16))
    gain_sums = lax.psum_scatter(gain_term, "intra", scatter_dimension=0, tiled=True)
    weight_grad, gain_grad = (
        lax.psum_scatter(term_low.astype(jnp.float32), "inter", scatter_dimension=0, tiled=True),
        lax.psum_scatter(gain_sums, "inter", scatter_dimension=0, tiled=True),
    )
    return (attn_flat.reshape(tokens_here, qcols)[None], grad_rows[None], weight_grad, gain_grad)


def solution(mesh):
    return jax.shard_map(
        local,
        mesh=mesh,
        in_specs=(
            P("inter", "intra", None),
            P(("inter", "intra")),
            P(("inter", "intra"), None),
            P("inter", "intra", None),
        ),
        out_specs=(
            P("inter", "intra", None),
            P("inter", "intra", None),
            P(("intra", "inter"), None),
            P(("intra", "inter")),
        ),
        check_vma=False,
    )
```

profile of v0, /device:TPU:0, one launch (start us, length us, event | category | flops | bytes accessed | tf_op | source)
XLA Modules:
  0.0 226.0 jit_solution(16348973796730813861)
XLA Ops:
  7.2 0.0 copy-start
  7.2 0.0 all-gather.6.cloned.1.call-start
  7.2 10.6 %all_gather.37 = bf16[256,768]{1,0:T(8,128)(2,1)} all-gather(bf16[128,768]{1,0:T(8,128)(2,1)} %param.6), channel_id=1, replica_groups=mesh['inter'=16,'intra'=2] {'intra'}, dimensions={0}, use_global_device_ids=true | all-gather | bytes 589824 | tf_op jit(solution)/shard_map/all_gather | solution.py:118
  17.8 0.0 all-gather.6.cloned.1.call-update
  17.8 4.4 %all-gather = bf16[2,1,128]{2,1,0:T(2,128)(2,1)S(1)} all-gather(bf16[1,1,128]{2,1,0:T(2,128)(2,1)} %bitcast.94), channel_id=1, replica_groups=mesh['inter'=16,'intra'=2] {'intra'}, dimensions={0}, use_global_device_ids=true | all-gather | bytes 768 | tf_op jit(solution)/shard_map/all_gather | solution.py:119
  22.2 22.1 %all-gather.1 = bf16[16,1,256]{2,1,0:T(2,128)(2,1)S(1)} all-gather(bf16[1,1,256]{2,1,0:T(2,128)(2,1)S(1)} %bitcast.93), channel_id=1, replica_groups=mesh['inter'=16,'intra'=2] {'inter'}, dimensions={0}, use_global_device_ids=true | all-gather | bytes 8704 | tf_op jit(solution)/shard_map/all_gather | solution.py:123
  44.3 3.1 %reshape.149 = f32[128,2,2048]{2,1,0:T(2,128)S(1)} reshape(bf16[1,128,4096]{2,1,0:T(8,128)(2,1)} %param.4) | data formatting | bytes 3145728 | tf_op jit(solution)/shard_map/convert_element_type | solution.py:130
  47.5 0.3 fusion
  47.8 0.6 multiply_multiply_fusion
  48.4 2.1 fusion.10
  50.5 3.6 %all-to-all-start = ((bf16[128,2,2048]{2,0,1:T(8,128)(2,1)}), bf16[128,2,2048]{2,0,1:T(8,128)(2,1)S(1)}, u32[]{:S(2)}, u32[]{:S(2)}) async-start(bf16[128,2,2048]{2,0,1:T(8,128)(2,1)} %fusion.10), calls=%async_computation | async-start | bytes 2097152 | tf_op jit(solution)/shard_map/all_to_all | solution.py:213
  54.1 0.0 reduce-scatter.2.cloned.1.call-start
  54.2 0.1 broadcast_in_dim.21
  54.3 0.7 le.15
  55.0 0.1 reshape_squeeze.3
  55.1 0.8 copy.18
  55.9 15.4 %all_gather.43 = bf16[1024,128]{1,0:T(8,128)(2,1)S(1)} all-gather(bf16[512,128]{1,0:T(8,128)(2,1)S(1)} %reshape_squeeze.3), channel_id=1, replica_groups=mesh['inter'=16,'intra'=2] {'intra'}, dimensions={0}, use_global_device_ids=true | all-gather | bytes 393216 | tf_op jit(solution)/shard_map/all_gather | solution.py:188
  71.3 0.6 add_select_fusion
  71.9 7.8 %all-gather.6.cloned.1.call-done = bf16[4096,768]{1,0:T(8,128)(2,1)} async-done(((bf16[256,768]{1,0:T(8,128)(2,1)}), bf16[4096,768]{1,0:T(8,128)(2,1)}) %all-gather.6.cloned.1.call-update) | async-done | bytes 6291472 | tf_op jit(solution)/shard_map/all_gather | solution.py:122
  79.7 3.8 %fusion.24 = f32[128,768]{1,0:T(8,128)S(1)} fusion(bf16[4096,768]{1,0:T(8,128)(2,1)} %all-gather.6.cloned.1.call-done, bf16[1,128,4096]{2,1,0:T(8,128)(2,1)S(1)} %copy-done, f32[4096]{0:T(1024)S(1)} %bitcast.86, f32[128]{0:T(128)} %copy-done.11), kind=kOutput, calls=%fused_computation.37 | convolution fusion | flops 807403520 | bytes 7750144 | tf_op jit(solution)/shard_map/dot_general | solution.py:133
  83.6 4.7 %all_gather.40 = bf16[256,128]{1,0:T(8,128)(2,1)} all-gather(bf16[128,128]{1,0:T(8,128)(2,1)S(1)} %slice.71), channel_id=1, replica_groups=mesh['inter'=16,'intra'=2] {'intra'}, dimensions={0}, use_global_device_ids=true | all-gather | bytes 98304 | tf_op jit(solution)/shard_map/all_gather | solution.py:160
  88.3 0.0 copy-done.13
  88.3 0.3 fusion.52
  88.6 0.1 pad_maximum_fusion.1
  88.7 0.6 copy-done.5
  89.4 4.7 %all_gather.39 = bf16[256,128]{1,0:T(8,128)(2,1)} all-gather(bf16[128,128]{1,0:T(8,128)(2,1)S(1)} %pad_maximum_fusion.1), channel_id=1, replica_groups=mesh['inter'=16,'intra'=2] {'intra'}, dimensions={0}, use_global_device_ids=true | all-gather | bytes 98304 | tf_op jit(solution)/shard_map/all_gather | solution.py:159
  94.0 0.1 reshape.146
  94.1 0.0 copy-start.8
  94.2 0.0 copy-start.9
  94.2 0.3 multiply_subtract_fusion.1
  94.5 0.1 fusion.32
  94.6 5.7 %all_gather.41 = bf16[1024,128]{1,0:T(8,128)(2,1)} all-gather(bf16[512,128]{1,0:T(8,128)(2,1)S(1)} %fusion.32), channel_id=1, replica_groups=mesh['inter'=16,'intra'=2] {'intra'}, dimensions={0}, use_global_device_ids=true | all-gather | bytes 393216 | tf_op jit(solution)/shard_map/all_gather | solution.py:187
  100.4 0.2 fusion.65
  100.6 0.1 fusion.31
  100.8 0.6 log_add_fusion
  101.4 1.1 multiply_reduce_fusion
  102.5 0.6 copy-done.15
  103.1 2.1 fusion.20
  105.2 4.7 %all-gather.2 = f32[2,1,512]{2,1,0:T(1,128)S(1)} all-gather(f32[1,1,512]{2,1,0:T(1,128)} %bitcast.90), channel_id=1, replica_groups=mesh['inter'=16,'intra'=2] {'intra'}, dimensions={0}, use_global_device_ids=true | all-gather | bytes 6144 | tf_op jit(solution)/shard_map/all_gather | solution.py:177
  109.9 5.3 %all-gather.3 = f32[2,1,512]{2,1,0:T(1,128)} all-gather(f32[1,1,512]{2,1,0:T(1,128)} %bitcast.92), channel_id=1, replica_groups=mesh['inter'=16,'intra'=2] {'intra'}, dimensions={0}, use_global_device_ids=true | all-gather | bytes 6144 | tf_op jit(solution)/shard_map/all_gather | solution.py:178
  115.2 2.0 multiply_add_fusion
  117.3 1.3 fusion.13
  118.6 0.9 convolution_convert_fusion.1
  119.5 1.8 fusion.21
  121.3 1.2 fusion.33
  122.6 0.9 copy.22
  123.4 1.2 fusion.56
  124.7 0.1 pad_maximum_fusion
  124.8 6.3 %all_gather.45 = bf16[256,768]{1,0:T(8,128)(2,1)S(1)} all-gather(bf16[128,768]{1,0:T(8,128)(2,1)S(1)} %pad_maximum_fusion), channel_id=1, replica_groups=mesh['inter'=16,'intra'=2] {'intra'}, dimensions={0}, use_global_device_ids=true | all-gather | bytes 589824 | tf_op jit(solution)/shard_map/all_gather | solution.py:216
  131.1 0.0 all-to-all-done
  131.1 1.0 convolution_convert_fusion
  132.2 3.1 %convert_element_type.81 = f32[2048,768]{1,0:T(8,128)} convert(bf16[2048,768]{1,0:T(8,128)(2,1)S(1)} %convolution_convert_fusion) | non-fusion elementwise | flops 1572864 | bytes 9437184 | tf_op jit(solution)/shard_map/convert_element_type | solution.py:223
  135.3 0.0 reduce-scatter.2.cloned.1.call-update
  135.3 0.6 copy-done.19
  135.9 0.6 dynamic-slice.2
  136.6 0.6 dynamic-slice
  138.4 0.1 copy.17
  138.6 0.7 broadcast_in_dim_reshape.2
  139.3 5.6 %fusion.8 = (f32[4096]{0:T(1024)S(1)}, f32[128]{0:T(128)S(1)}, f32[128,4096]{1,0:T(8,128)S(1)}) fusion(bf16[1,128,4096]{2,1,0:T(8,128)(2,1)S(1)} %copy-done, f32[128]{0:T(128)S(1)} %copy-done.12, f32[4096]{0:T(1024)S(1)} %bitcast.87, bf16[128,768]{1,0:T(8,128)(2,1)S(1)} %pad_maximum_fusion, bf16[4096,768]{1,0:T(8,128)(2,1)} %all-gather.6.cloned.1.call-done), kind=kOutput, calls=%fused_computation.14 | convolution fusion | flops 808972160 | bytes 9667584 | tf_op jit(solution)/shard_map/tc,dc->td/dot_general | solution.py:205
  144.9 7.1 %all-reduce = f32[4096]{0:T(1024)S(1)} all-reduce(f32[4096]{0:T(1024)S(1)} %get-tuple-element.4), channel_id=3, replica_groups=mesh['inter'=16,'intra'=2] {'intra'}, use_global_device_ids=true, to_apply=%region_7.8.clone | all-reduce | flops 4096 | bytes 32768
  152.1 30.9 %all-reduce.1 = f32[2048]{0:T(1024)S(1)} all-reduce(f32[2048]{0:T(1024)S(1)} %dynamic-slice.1), channel_id=4, replica_groups=mesh['inter'=16,'intra'=2] {'inter'}, use_global_device_ids=true, to_apply=%region_8.9.clone | all-reduce | flops 2048 | bytes 16384
  183.0 0.6 dynamic-slice.3
  183.6 1.6 fusion.23
  185.2 34.0 %reduce-scatter.2.cloned.1.call-done = f32[128,768]{1,0:T(8,128)} async-done(((f32[2048,768]{1,0:T(8,128)}), f32[128,768]{1,0:T(8,128)}) %reduce-scatter.2.cloned.1.call-update) | async-done | bytes 393232 | tf_op jit(solution)/shard_map/reduce_scatter | solution.py:223
  (45 shorter events, 0.2 us)
Async XLA Ops:
  7.2 40.3 %copy-start = (bf16[1,128,4096]{2,1,0:T(8,128)(2,1)S(1)}, bf16[1,128,4096]{2,1,0:T(8,128)(2,1)}, u32[]{:S(2)}) copy-start(bf16[1,128,4096]{2,1,0:T(8,128)(2,1)} %param.4) | copy-start | bytes 3145732
  7.2 72.5 %all-gather.6.cloned.1.call-start = ((), (), s32[]{:S(2)}) async-start(), calls=%async_computation.2 | async-start | bytes 6684672 | tf_op jit(solution)/shard_map/all_gather | solution.py:122
  48.4 2.1 copy-start.11
  48.4 6.6 %copy-start.6 = (bf16[1,128,512]{2,1,0:T(8,128)(2,1)S(1)}, bf16[1,128,512]{2,1,0:T(8,128)(2,1)}, u32[]{:S(2)}) copy-start(bf16[1,128,512]{2,1,0:T(8,128)(2,1)} %param.7) | copy-start | bytes 393220
  50.5 80.6 %all-to-all-start = ((bf16[128,2,2048]{2,0,1:T(8,128)(2,1)}), bf16[128,2,2048]{2,0,1:T(8,128)(2,1)S(1)}, u32[]{:S(2)}, u32[]{:S(2)}) async-start(bf16[128,2,2048]{2,0,1:T(8,128)(2,1)} %fusion.10), calls=%async_computation | async-start | bytes 2097152 | tf_op jit(solution)/shard_map/all_to_all | solution.py:213
  54.1 165.0 %reduce-scatter.2.cloned.1.call-start = ((), (), s32[]{:S(2)}) async-start(), calls=%async_computation.3 | async-start | bytes 6684672 | tf_op jit(solution)/shard_map/reduce_scatter | solution.py:223
  54.2 0.9 copy-start.17
  71.3 17.0 %copy-start.13 = (f32[128]{0:T(128)}, f32[128]{0:T(128)S(1)}, u32[]{:S(2)}) copy-start(f32[128]{0:T(128)S(1)} %fusion.64) | copy-start | bytes 1540
  71.3 17.0 %copy-start.14 = (f32[64]{0:T(128)}, f32[64]{0:T(128)S(1)}, u32[]{:S(2)}) copy-start(f32[64]{0:T(128)S(1)} %multiply_power_fusion) | copy-start | bytes 772
  88.6 12.1 %copy-start.2 = (f32[128,64]{1,0:T(8,128)}, f32[128,64]{1,0:T(8,128)S(1)}, u32[]{:S(2)}) copy-start(f32[128,64]{1,0:T(8,128)S(1)} %get-tuple-element.14) | copy-start | bytes 98308
  88.6 12.1 %copy-start.3 = (f32[128,64]{1,0:T(8,128)}, f32[128,64]{1,0:T(8,128)S(1)}, u32[]{:S(2)}) copy-start(f32[128,64]{1,0:T(8,128)S(1)} %get-tuple-element.15) | copy-start | bytes 98308
  88.7 0.6 copy-start.5
  94.1 6.2 %copy-start.4 = (bf16[256,128]{1,0:T(8,128)(2,1)S(1)}, bf16[256,128]{1,0:T(8,128)(2,1)}, u32[]{:S(2)}) copy-start(bf16[256,128]{1,0:T(8,128)(2,1)} %all_gather.39) | copy-start | bytes 196612
  94.1 6.2 %copy-start.10 = (s32[512]{0:T(512)S(1)}, s32[512]{0:T(512)}, u32[]{:S(2)}) copy-start(s32[512]{0:T(512)} %le.15) | copy-start | bytes 6148
  94.1 7.2 %copy-start.8 = (bf16[512,128]{0,1:T(8,128)(2,1)S(1)}, bf16[512,128]{0,1:T(8,128)(2,1)}, u32[]{:S(2)}) copy-start(bf16[512,128]{0,1:T(8,128)(2,1)} %copy.18) | copy-start | bytes 393220
  94.2 7.2 %copy-start.9 = (bf16[256,128]{1,0:T(8,128)(2,1)S(1)}, bf16[256,128]{1,0:T(8,128)(2,1)}, u32[]{:S(2)}) copy-start(bf16[256,128]{1,0:T(8,128)(2,1)} %all_gather.40) | copy-start | bytes 196612
  102.5 0.6 copy-start.15
  105.2 14.3 %copy-start.1 = (bf16[1024,128]{1,0:T(8,128)(2,1)S(1)}, bf16[1024,128]{1,0:T(8,128)(2,1)}, u32[]{:S(2)}) copy-start(bf16[1024,128]{1,0:T(8,128)(2,1)} %all_gather.41) | copy-start | bytes 786436
  135.3 0.7 copy-start.19
  135.3 1.3 copy-start.18
  135.3 3.1 %copy-start.7 = (bf16[512,128]{0,1:T(8,128)(2,1)S(1)}, bf16[512,128]{0,1:T(8,128)(2,1)}, u32[]{:S(2)}) copy-start(bf16[512,128]{0,1:T(8,128)(2,1)} %get-tuple-element.21) | copy-start | bytes 393220
  135.3 4.0 %copy-start.12 = (f32[128]{0:T(128)S(1)}, f32[128]{0:T(128)}, u32[]{:S(2)}) copy-start(f32[128]{0:T(128)} %copy-done.11) | copy-start | bytes 1540
  139.3 44.3 %copy-start.16 = (f32[128]{0:T(128)S(1)}, f32[128]{0:T(128)}, u32[]{:S(2)}) copy-start(f32[128]{0:T(128)} %get-tuple-element.16) | copy-start | bytes 1540
Sparse Core Ops, SparseCore 0:
  17.9 61.7 all-gather.5
  135.4 83.6 reduce-scatter.1
where the time goes:
time: 227 us; the launch traced here: 226 us
  blocking collectives  122 us (54%)
  waiting for transfers between devices  41.8 us (18%)
  matrix products  18 us (8%)
  between operations  15.7 us (7%)
  other arithmetic  14.6 us (6%)
  local copies, waits for them, and re-layouts  10.3 us (5%)
  starting transfers between devices  3.67 us (2%)
    unnamed x2, blocking collectives  38.1 us
    reduce_scatter x1, waiting for transfers between devices, local(): lax.psum_scatter(term_low.astype(jnp.float32), 'inter', scatter_dimension...  34 us
    all_gather x1, blocking collectives, local(): lax.all_gather(gain_group, 'inter', axis=0, tiled=True)  22.1 us
    all_gather x1, blocking collectives, local(): lax.all_gather(grad_flat, 'intra', axis=0, tiled=True)  15.4 us
    all_gather x1, blocking collectives, local(): lax.all_gather(qkv_weight, 'intra', axis=0, tiled=True)  10.6 us
    all_gather x1, waiting for transfers between devices, local(): lax.all_gather(weight_group, 'inter', axis=0, tiled=True)  7.82 us
    all_gather x1, blocking collectives, local(): lax.all_gather(grad_mixed, 'intra', axis=0, tiled=True)  6.34 us
    all_gather x1, blocking collectives, local(): lax.all_gather(query_rows, 'intra', axis=0, tiled=True)  5.74 us
  transfers between devices with their start and end apart: 3, of which 2 were waited for; matrix products, arithmetic and copies ran while one was open for 16% of the time, Pallas kernels for 0%

commit v1 on v0

--- a/solution.py
+++ b/solution.py
@@ -1,6 +1,10 @@
+import functools
 import jax
 import jax.numpy as jnp
+import numpy as np
 from jax import lax
+from jax.experimental import pallas as pl
+from jax.experimental.pallas import tpu as pltpu
 from jax.sharding import PartitionSpec as P
 
 HD = 128
@@ -225,10 +229,377 @@
     )
     return (attn_flat.reshape(tokens_here, qcols)[None], grad_rows[None], weight_grad, gain_grad)
 
+MESH = pl.DeviceIdType.MESH
+CORES = 2
+SIDE = 2
+GAIN_ROWS = 16
+
+
+def nt_dot(a, b):
+    return lax.dot_general(a, b, (((1,), (1,)), ((), ())), preferred_element_type=jnp.float32)
+
+
+def tn_dot(a, b):
+    return lax.dot_general(a, b, (((0,), (0,)), ((), ())), preferred_element_type=jnp.float32)
+
+
+def nn_dot(a, b):
+    return jnp.dot(a, b, preferred_element_type=jnp.float32)
+
+
+def fused_kernel(
+    n_inter,
+    hid_ref, gain_ref, w_ref, ct_ref, cos_ref, sin_ref,
+    attn_ref, gin_ref, wg_ref, gg_ref,
+    wbuf, nrm, nbuf, kvbuf, gkv, gkv_in, gmbuf, tbuf, rs1, ybuf, rs2, zbuf, rs3, mix,
+    ag_send, ag_recv, ex_send, ex_recv, c_send, c_recv, y_send, y_recv, z_send, z_recv,
+):
+    i = lax.axis_index("inter")
+    x = lax.axis_index("intra")
+    nz = n_inter // (CORES * SIDE)
+    c = lax.rem(i, CORES)
+    y = lax.rem(i // CORES, SIDE)
+    z = i // (CORES * SIDE)
+    toks, width = hid_ref.shape
+    rows, cols = w_ref.shape
+    half = width // 2
+    qcols = HEADS * HD
+    scale = HD ** (-0.5)
+
+    def dev(zz, yy, cc, xx):
+        return ((zz * SIDE + yy) * CORES + cc, xx)
+
+    def slot(zz, yy, cc, xx):
+        return ((zz * SIDE + yy) * CORES + cc) * 2 + xx
+
+    x_peer = dev(z, y, c, 1 - x)
+    y_peer = dev(z, 1 - y, c, x)
+    c_peer = dev(z, y, 1 - c, x)
+
+    def z_peer(zz):
+        return dev(zz, y, c, x)
+
+    own = slot(z, y, c, x)
+    wbuf[own, :rows, :] = w_ref[...]
+    wbuf[own, rows:, :HD] = jnp.broadcast_to(gain_ref[...], (GAIN_ROWS, HD))
+    wbuf[own, rows:, HD:] = jnp.zeros((GAIN_ROWS, cols - HD), jnp.bfloat16)
+
+    barrier = pltpu.get_barrier_semaphore()
+    peers = [x_peer, y_peer, c_peer] + [z_peer(lax.rem(z + d, nz)) for d in range(1, nz)]
+    for peer in peers:
+        pl.semaphore_signal(barrier, inc=1, device_id=peer, device_id_type=MESH)
+    pl.semaphore_wait(barrier, len(peers))
+
+    targets = {
+        0: x_peer,
+        1: y_peer,
+        2: z_peer(jnp.minimum(z + 1, nz - 1)),
+        3: z_peer(jnp.maximum(z - 1, 0)),
+        4: c_peer,
+    }
+    sent = []
+
+    def ag(link, g):
+        return pltpu.make_async_remote_copy(
+            src_ref=wbuf.at[g], dst_ref=wbuf.at[g],
+            send_sem=ag_send.at[link, g], recv_sem=ag_recv.at[g],
+            device_id=targets[link], device_id_type=MESH,
+        )
+
+    def send(link, g, cond=None):
+        sent.append((link, g, cond))
+        if cond is None:
+            ag(link, g).start()
+        else:
+            pl.when(cond)(lambda: ag(link, g).start())
+
+    def arrive(g, cond=None):
+        if cond is None:
+            ag(0, g).wait_recv()
+        else:
+            pl.when(cond)(lambda: ag(0, g).wait_recv())
+
+    def both(a, b):
+        return b if a is None else jnp.logical_and(a, b)
+
+    up, down = z < nz - 1, z > 0
+    send(0, own)
+    send(1, own)
+    send(2, own, up)
+    send(3, own, down)
+    send(4, own)
+    wide = hid_ref[...].astype(jnp.float32)
+    inv = lax.rsqrt(jnp.mean(wide * wide, axis=1, keepdims=True) + eps_norm)
+    for d in range(nz):
+        sides = [(z, None, None)] if d == 0 else [(z - d, z - d >= 0, 2), (z + d, z + d < nz, 3)]
+        if d > 0:
+            for zz, ok, link in sides:
+                g = slot(zz, y, c, x)
+                arrive(g, ok)
+                send(link, g, both(ok, up if link == 2 else down))
+                send(0, g, ok)
+                send(1, g, ok)
+                send(4, g, ok)
+        for zz, ok, link in sides:
+            odd = lax.rem(zz + 2 * nz, 2) == 1
+            g = slot(zz, y, c, 1 - x)
+            arrive(g, ok)
+            send(1, g, both(ok, odd))
+            send(4, g, ok)
+            g = slot(zz, 1 - y, c, x)
+            arrive(g, ok)
+            send(0, g, both(ok, jnp.logical_not(odd)))
+            send(4, g, ok)
+    for zz in range(nz):
+        g = slot(zz, 1 - y, c, 1 - x)
+        arrive(g)
+        send(4, g)
+    for zz in range(nz):
+        for yy in range(SIDE):
+            for xx in range(2):
+                arrive(slot(zz, yy, 1 - c, xx))
+
+    acc = jnp.zeros((toks, cols), jnp.float32)
+    for p in range(n_inter):
+        parts = []
+        for q in range(2):
+            g = 2 * p + q
+            lanes = slice(g * rows, (g + 1) * rows)
+            gain = wbuf[g, rows : rows + 1, :rows].astype(jnp.float32)
+            part = (hid_ref[:, lanes].astype(jnp.float32) * inv * gain).astype(jnp.bfloat16)
+            nrm[:, lanes] = part
+            parts.append(part)
+        acc = acc + nn_dot(
+            jnp.concatenate(parts, axis=1),
+            jnp.concatenate([wbuf[2 * p, :rows, :], wbuf[2 * p + 1, :rows, :]], axis=0),
+        )
+    mix[...] = acc
+
+    cosine = cos_ref[pl.ds(pl.multiple_of(x * toks, toks), toks), :]
+    sine = sin_ref[pl.ds(pl.multiple_of(x * toks, toks), toks), :]
+
+    def rope(u):
+        return u * cosine + pltpu.roll(u, HD // 2, 1) * sine
+
+    def unrope(u):
+        return u * cosine - pltpu.roll(u, HD // 2, 1) * sine
+
+    here = pl.ds(pl.multiple_of(x * toks, toks), toks)
+    there = pl.ds(pl.multiple_of((1 - x) * toks, toks), toks)
+
+    def exchange(k, src, dst):
+        return pltpu.make_async_remote_copy(
+            src_ref=src, dst_ref=dst, send_sem=ex_send.at[k], recv_sem=ex_recv.at[k],
+            device_id=x_peer, device_id_type=MESH,
+        )
+
+    kvbuf[here, :HD] = rope(acc[:, qcols : qcols + HD]).astype(jnp.bfloat16)
+    kvbuf[here, HD:] = acc[:, qcols + HD :].astype(jnp.bfloat16)
+    query = [(rope(acc[:, h * HD : (h + 1) * HD]) * scale).astype(jnp.bfloat16) for h in range(HEADS)]
+    query = jnp.concatenate(query, axis=0)
+    kv_copy = exchange(0, kvbuf.at[here], kvbuf.at[here])
+    kv_copy.start()
+    keep = pl.ds(pl.multiple_of(x * half, half), half)
+    give = pl.ds(pl.multiple_of((1 - x) * half, half), half)
+    norm_copy = exchange(1, nrm.at[:, give], nbuf.at[here])
+    norm_copy.start()
+    nbuf[here, :] = nrm[:, keep]
+    kv_copy.wait()
+
+    flat = HEADS * toks
+    keys, values = kvbuf[:, :HD], kvbuf[:, HD:]
+    row_pos = x * toks + lax.rem(lax.broadcasted_iota(jnp.int32, (flat, 2 * toks), 0), toks)
+    allowed = lax.broadcasted_iota(jnp.int32, (flat, 2 * toks), 1) <= row_pos
+    scores = jnp.where(allowed, nt_dot(query, keys), -1e30)
+    top = jnp.max(scores, axis=1, keepdims=True)
+    numbers = jnp.where(allowed, jnp.exp(scores - top), 0.0)
+    total = jnp.sum(numbers, axis=1, keepdims=True)
+    high = numbers.astype(jnp.bfloat16)
+    low = (numbers - high.astype(jnp.float32)).astype(jnp.bfloat16)
+    attn = ((nn_dot(high, values) + nn_dot(low, values)) / total).astype(jnp.bfloat16)
+    for h in range(HEADS):
+        attn_ref[:, h * HD : (h + 1) * HD] = attn[h * toks : (h + 1) * toks]
+    grad = jnp.concatenate([ct_ref[:, h * HD : (h + 1) * HD] for h in range(HEADS)], axis=0)
+    delta = jnp.sum(grad.astype(jnp.float32) * attn.astype(jnp.float32), axis=1, keepdims=True)
+    probs = numbers / total
+    grad_scores = (probs * (nt_dot(grad, values) - delta)).astype(jnp.bfloat16)
+    gkv[:, :HD] = tn_dot(grad_scores, query)
+    gkv[:, HD:] = tn_dot(probs.astype(jnp.bfloat16), grad)
+    gkv_copy = exchange(2, gkv.at[there], gkv_in)
+    gkv_copy.start()
+    grad_query = nn_dot(grad_scores, keys)
+    for h in range(HEADS):
+        gmbuf[here, h * HD : (h + 1) * HD] = (
+            unrope(grad_query[h * toks : (h + 1) * toks]) * scale
+        ).astype(jnp.bfloat16)
+    gkv_copy.wait()
+    own_kv = gkv[here, :] + gkv_in[...]
+    gmbuf[here, qcols : qcols + HD] = unrope(own_kv[:, :HD]).astype(jnp.bfloat16)
+    gmbuf[here, qcols + HD :] = own_kv[:, HD:].astype(jnp.bfloat16)
+    gm_copy = exchange(3, gmbuf.at[here], gmbuf.at[here])
+    gm_copy.start()
+
+    gm = gmbuf[here, :]
+    inner = jnp.sum(gm.astype(jnp.float32) * mix[...], axis=1, keepdims=True)
+    back = inner * (inv * inv / width)
+
+    def grad_rows(first, last):
+        for g in range(first, last):
+            lanes = slice(g * rows, (g + 1) * rows)
+            gain = wbuf[g, rows : rows + 1, :rows].astype(jnp.float32)
+            part = nt_dot(gm, wbuf[g, :rows, :])
+            gin_ref[:, lanes] = (
+                gain * part * inv - hid_ref[:, lanes].astype(jnp.float32) * back
+            ).astype(jnp.bfloat16)
+
+    pieces = nz + 1
+    marks = [2 * n_inter * k // pieces for k in range(pieces + 1)]
+    grad_rows(marks[0], marks[1])
+    norm_copy.wait()
+    gm_copy.wait()
+
+    both_gm = gmbuf[...]
+
+    def term(k, cc):
+        j = k * CORES + cc
+        lanes = pl.ds(pl.multiple_of(j * rows, rows), rows)
+        tbuf[j] = tn_dot(nbuf[:, lanes], both_gm).astype(jnp.bfloat16)
+
+    def to_core(k):
+        return pltpu.make_async_remote_copy(
+            src_ref=tbuf.at[k * CORES + 1 - c], dst_ref=rs1.at[k],
+            send_sem=c_send.at[k], recv_sem=c_recv.at[k], device_id=c_peer, device_id_type=MESH,
+        )
+
+    def to_y(zz):
+        return pltpu.make_async_remote_copy(
+            src_ref=ybuf.at[zz], dst_ref=rs2.at[zz],
+            send_sem=y_send.at[zz], recv_sem=y_recv.at[zz], device_id=y_peer, device_id_type=MESH,
+        )
+
+    def to_z(d):
+        return pltpu.make_async_remote_copy(
+            src_ref=zbuf.at[d - 1], dst_ref=rs3.at[d - 1],
+            send_sem=z_send.at[d - 1], recv_sem=z_recv.at[d - 1],
+            device_id=z_peer(lax.rem(z + d, nz)), device_id_type=MESH,
+        )
+
+    order = [(d, lax.rem(z + d, nz)) for d in list(range(1, nz)) + [0]]
+
+    def core_sum(k):
+        to_core(k).wait_recv()
+        return tbuf[k * CORES + c].astype(jnp.float32) + rs1[k].astype(jnp.float32)
+
+    for yy in (1 - y, y):
+        for d, zz in order:
+            term(zz * SIDE + yy, 1 - c)
+            to_core(zz * SIDE + yy).start()
+            term(zz * SIDE + yy, c)
+            if yy is not y:
+                pass
+        if yy is not y:
+            for d, zz in order:
+                ybuf[zz] = core_sum(zz * SIDE + yy).astype(jnp.bfloat16)
+                to_y(zz).start()
+    kept = None
+    for n, (d, zz) in enumerate(order):
+        grad_rows(marks[n + 1], marks[n + 2])
+        part = core_sum(zz * SIDE + y)
+        to_y(zz).wait_recv()
+        part = part + rs2[zz].astype(jnp.float32)
+        if d:
+            zbuf[d - 1] = part.astype(jnp.bfloat16)
+            to_z(d).start()
+        else:
+            wg_ref[...] = part
+    result = wg_ref[...]
+    for d in range(1, nz):
+        to_z(d).wait_recv()
+        result = result + rs3[d - 1].astype(jnp.float32)
+    wg_ref[...] = result
+    block = x * n_inter + i
+    mixed_sum = wbuf[block, :rows, :].astype(jnp.float32) * result
+    lanes_sum = mixed_sum[:, :HD]
+    for k in range(1, cols // HD):
+        lanes_sum = lanes_sum + mixed_sum[:, k * HD : (k + 1) * HD]
+    gain = wbuf[block, rows : rows + 1, :rows].astype(jnp.float32)
+    gg_ref[...] = jnp.sum(lanes_sum.T, axis=0, keepdims=True) / gain
+
+    for link, g, cond in sent:
+        if cond is None:
+            ag(link, g).wait_send()
+        else:
+            pl.when(cond)(functools.partial(lambda l, s: ag(l, s).wait_send(), link, g))
+    for k in range(nz * SIDE):
+        to_core(k).wait_send()
+    for zz in range(nz):
+        to_y(zz).wait_send()
+    for d in range(1, nz):
+        to_z(d).wait_send()
+
+
+def fused(n_inter, hidden_in, norm_gain, qkv_weight, attn_cotangent):
+    toks, width = hidden_in.shape[1:]
+    rows, cols = qkv_weight.shape
+    nz = n_inter // (CORES * SIDE)
+    chips = nz * SIDE
+    freqs = rope_base ** (-np.arange(HD // 2, dtype=np.float32) / np.float32(HD // 2))
+    angles = (np.arange(2 * toks, dtype=np.float32)[:, None] * freqs.astype(np.float32)[None, :]).astype(np.float32)
+    cosine = np.concatenate([np.cos(angles)] * 2, axis=1).astype(np.float32)
+    sine = np.concatenate([-np.sin(angles), np.sin(angles)], axis=1).astype(np.float32)
+    bf, f32, dma = jnp.bfloat16, jnp.float32, pltpu.SemaphoreType.DMA
+    vmem = pl.BlockSpec(memory_space=pltpu.VMEM)
+    attn, gin, wg, gg = pl.pallas_call(
+        functools.partial(fused_kernel, n_inter),
+        out_shape=(
+            jax.ShapeDtypeStruct((toks, HEADS * HD), bf),
+            jax.ShapeDtypeStruct((toks, width), bf),
+            jax.ShapeDtypeStruct((rows, cols), f32),
+            jax.ShapeDtypeStruct((1, rows), f32),
+        ),
+        in_specs=[vmem] * 6,
+        out_specs=(vmem,) * 4,
+        scratch_shapes=[
+            pltpu.VMEM((2 * n_inter, rows + GAIN_ROWS, cols), bf),
+            pltpu.VMEM((toks, width), bf),
+            pltpu.VMEM((2 * toks, width // 2), bf),
+            pltpu.VMEM((2 * toks, 2 * HD), bf),
+            pltpu.VMEM((2 * toks, 2 * HD), f32),
+            pltpu.VMEM((toks, 2 * HD), f32),
+            pltpu.VMEM((2 * toks, cols), bf),
+            pltpu.VMEM((n_inter, rows, cols), bf),
+            pltpu.VMEM((chips, rows, cols), bf),
+            pltpu.VMEM((nz, rows, cols), bf),
+            pltpu.VMEM((nz, rows, cols), bf),
+            pltpu.VMEM((max(nz - 1, 1), rows, cols), bf),
+            pltpu.VMEM((max(nz - 1, 1), rows, cols), bf),
+            pltpu.VMEM((toks, cols), f32),
+            dma((5, 2 * n_inter)), dma((2 * n_inter,)),
+            dma((4,)), dma((4,)),
+            dma((chips,)), dma((chips,)),
+            dma((nz,)), dma((nz,)),
+            dma((max(nz - 1, 1),)), dma((max(nz - 1, 1),)),
+        ],
+        compiler_params=pltpu.CompilerParams(
+            collective_id=0, has_side_effects=True, vmem_limit_bytes=60 * 2**20
+        ),
+    )(hidden_in[0], norm_gain[None], qkv_weight, attn_cotangent[0], cosine, sine)
+    return attn[None], gin[None], wg, gg[0]
+
 
 def solution(mesh):
+    n_inter, n_intra = mesh.shape["inter"], mesh.shape["intra"]
+
+    def body(hidden_in, norm_gain, qkv_weight, attn_cotangent):
+        fits = n_intra == 2 and n_inter % (CORES * SIDE) == 0
+        fits = fits and qkv_weight.shape[0] == HD and hidden_in.shape[0] == 1
+        fits = fits and hidden_in.shape[1] % HD == 0
+        if fits:
+            return fused(n_inter, hidden_in, norm_gain, qkv_weight, attn_cotangent)
+        return local(hidden_in, norm_gain, qkv_weight, attn_cotangent)
+
     return jax.shard_map(
-        local,
+        body,
         mesh=mesh,
         in_specs=(
             P("inter", "intra", None),

time: 227 us -> 106 us (0.47)
  blocking collectives: 122 us -> 0 us
  Pallas kernels: 0 us -> 98.9 us
  waiting for transfers between devices: 41.8 us -> 0 us
  matrix products: 18 us -> 0 us
  between operations: 15.7 us -> 0.64 us
  other arithmetic: 14.6 us -> 0 us
  local copies, waits for them, and re-layouts: 10.3 us -> 5.17 us
  starting transfers between devices: 3.67 us -> 0 us
    pallas_call x0 -> x1, Pallas kernels: none -> 98.9 us  [fused(): pl.pallas_call(functools.partial(fused_kernel, n_inter), out_shape=(jax.S...]
    all_gather x10 -> x0, blocking collectives: 83.9 us -> none  [the longest x1 22.1 us: local(): lax.all_gather(gain_group, 'inter', axis=0, tiled=True)]
    unnamed x2 -> x0, blocking collectives: 38.1 us -> none
    reduce_scatter x1 -> x0, waiting for transfers between devices: 34 us -> none  [local(): lax.psum_scatter(term_low.astype(jnp.float32), 'inter', scatter_dimension...]
    dot_general x9 -> x0, matrix products: 18 us -> none  [the longest x1 5.61 us: local(): jnp.einsum('tc,dc->td', grad_mixed, weight_back, preferred_element_type=j...]
    all_gather x1 -> x0, waiting for transfers between devices: 7.82 us -> none  [local(): lax.all_gather(weight_group, 'inter', axis=0, tiled=True)]
    convert_element_type x6 -> x0, other arithmetic: 5.46 us -> none  [the longest x1 3.13 us: local(): term_low.astype(jnp.float32)]
    all_to_all x1 -> x0, starting transfers between devices: 3.59 us -> none  [local(): lax.all_to_all(normed, 'intra', split_axis=1, concat_axis=0, tiled=True)]
  transfers between devices with their start and end apart: 3 -> 0, of which waited for: 2 -> 0; matrix products, arithmetic and copies ran while one was open for 16% -> 0% of each run, Pallas kernels for 0% -> 0%
where the time goes in v1:
time: 106 us; the launch traced here: 105 us
  Pallas kernels  98.9 us (93%)
  local copies, waits for them, and re-layouts  5.17 us (5%)
    pallas_call x1, Pallas kernels, fused(): pl.pallas_call(functools.partial(fused_kernel, n_inter), out_shape=(jax.S...  98.9 us
    unnamed x8, local copies, waits for them, and re-layouts  5.17 us

profile of v1, /device:TPU:0, one launch (start us, length us, event | category | flops | bytes accessed | tf_op | source)
XLA Modules:
  0.0 104.7 jit_solution(7213170279653862054)
XLA Ops:
  0.6 98.9 %shard_map.93 = (bf16[128,512]{1,0:T(8,128)(2,1)}, bf16[128,4096]{1,0:T(8,128)(2,1)}, f32[128,768]{1,0:T(8,128)}, f32[1,128]{1,0:T(1,128)}) custom-call(bf16[128,4096]{1,0:T(8,128)(2,1)} %bitcast.6, bf16[1,128]{1,0:T(2,128)(2,1)} %bitcast.10, bf16[128,768]{1,0:T(8,128)(2,1)} %w_ref.1, bf16[128,512]{1,0:T(8,128)(2,1)} %bitcast.8, ...), custom_call_target="tpu_custom_call" | custom-call | tf_op jit(solution)/shard_map/pallas_call | solution.py:552
  99.6 1.6 %copy.14 = bf16[1,128,512]{2,1,0:T(8,128)(2,1)} copy(bf16[1,128,512]{2,1,0:T(8,128)(2,1)} %bitcast.9) | data formatting | bytes 262144
  101.1 0.0 copy-start
  101.1 2.3 %copy.15 = bf16[1,128,4096]{2,1,0:T(8,128)(2,1)} copy(bf16[1,128,4096]{2,1,0:T(8,128)(2,1)} %bitcast.7) | data formatting | bytes 2097152
  103.5 0.0 copy-done
  103.5 0.0 copy-start.1
  103.5 0.7 copy.16
  104.2 0.0 copy-done.1
  104.2 0.5 copy.17
Async XLA Ops:
  101.1 2.3 %copy-start = (f32[128,768]{1,0:T(8,128)S(1)}, f32[128,768]{1,0:T(8,128)}, u32[]{:S(2)}) copy-start(f32[128,768]{1,0:T(8,128)} %get-tuple-element.18) | copy-start | bytes 1179652
  103.5 0.8 copy-start.1

commit v2 on v1

--- a/solution.py
+++ b/solution.py
@@ -330,50 +330,95 @@
     send(4, own)
     wide = hid_ref[...].astype(jnp.float32)
     inv = lax.rsqrt(jnp.mean(wide * wide, axis=1, keepdims=True) + eps_norm)
-    for d in range(nz):
-        sides = [(z, None, None)] if d == 0 else [(z - d, z - d >= 0, 2), (z + d, z + d < nz, 3)]
-        if d > 0:
-            for zz, ok, link in sides:
-                g = slot(zz, y, c, x)
-                arrive(g, ok)
-                send(link, g, both(ok, up if link == 2 else down))
-                send(0, g, ok)
-                send(1, g, ok)
-                send(4, g, ok)
-        for zz, ok, link in sides:
+    mix[...] = jnp.zeros((toks, cols), jnp.float32)
+    span = lambda g: pl.ds(pl.multiple_of(g * rows, rows), rows)
+
+    def absorb(g):
+        gain = wbuf[g, rows : rows + 1, :rows].astype(jnp.float32)
+        part = (hid_ref[:, span(g)].astype(jnp.float32) * inv * gain).astype(jnp.bfloat16)
+        nrm[:, span(g)] = part
+        mix[...] += nn_dot(part, wbuf[g, :rows, :])
+
+    def absorb_when(g, cond):
+        if cond is None:
+            absorb(g)
+        else:
+            pl.when(cond)(lambda: absorb(g))
+
+    def sides(d):
+        if d == 0:
+            return [(z, None, None)]
+        return [(z - d, z - d >= 0, 2), (z + d, z + d < nz, 3)]
+
+    def onward(link):
+        return up if link == 2 else down
+
+    late = []
+
+    def done(zz, yy, xx, ok):
+        late.append((zz, yy, xx, ok))
+        absorb_when(slot(zz, yy, c, xx), ok)
+
+    def drain(count):
+        for _ in range(min(count, len(late))):
+            zz, yy, xx, ok = late.pop(0)
+            g = slot(zz, yy, 1 - c, xx)
+            arrive(g, ok)
+            absorb_when(g, ok)
+
+    def column(d):
+        for zz, ok, link in sides(d):
+            g = slot(zz, y, c, x)
+            arrive(g, ok)
+            send(link, g, both(ok, onward(link)))
+            for k in (0, 1, 4):
+                send(k, g, ok)
+        for zz, ok, link in sides(d):
+            done(zz, y, x, ok)
+
+    direct = [d for d in range(nz) if d == 0 or d >= 3]
+
+    def side(d):
+        for zz, ok, link in sides(d):
             odd = lax.rem(zz + 2 * nz, 2) == 1
             g = slot(zz, y, c, 1 - x)
             arrive(g, ok)
-            send(1, g, both(ok, odd))
+            if d in direct:
+                send(1, g, both(ok, odd))
             send(4, g, ok)
             g = slot(zz, 1 - y, c, x)
             arrive(g, ok)
-            send(0, g, both(ok, jnp.logical_not(odd)))
+            if d in direct:
+                send(0, g, both(ok, jnp.logical_not(odd)))
             send(4, g, ok)
-    for zz in range(nz):
-        g = slot(zz, 1 - y, c, 1 - x)
-        arrive(g)
-        send(4, g)
-    for zz in range(nz):
-        for yy in range(SIDE):
-            for xx in range(2):
-                arrive(slot(zz, yy, 1 - c, xx))
-
-    acc = jnp.zeros((toks, cols), jnp.float32)
-    for p in range(n_inter):
-        parts = []
-        for q in range(2):
-            g = 2 * p + q
-            lanes = slice(g * rows, (g + 1) * rows)
-            gain = wbuf[g, rows : rows + 1, :rows].astype(jnp.float32)
-            part = (hid_ref[:, lanes].astype(jnp.float32) * inv * gain).astype(jnp.bfloat16)
-            nrm[:, lanes] = part
-            parts.append(part)
-        acc = acc + nn_dot(
-            jnp.concatenate(parts, axis=1),
-            jnp.concatenate([wbuf[2 * p, :rows, :], wbuf[2 * p + 1, :rows, :]], axis=0),
-        )
-    mix[...] = acc
+        for zz, ok, link in sides(d):
+            done(zz, y, 1 - x, ok)
+            done(zz, 1 - y, x, ok)
+
+    def diagonal(d):
+        for zz, ok, link in sides(d):
+            g = slot(zz, 1 - y, c, 1 - x)
+            arrive(g, ok)
+            if d + 1 < nz and d + 1 not in direct:
+                if d == 0:
+                    send(2, g, up)
+                    send(3, g, down)
+                else:
+                    send(link, g, both(ok, onward(link)))
+            send(4, g, ok)
+        for zz, ok, link in sides(d):
+            done(zz, 1 - y, 1 - x, ok)
+
+    done(z, y, x, None)
+    steps = [(d * 3, column, d) for d in range(1, nz)]
+    steps += [(d * 3 + 4, side, d) for d in range(nz)]
+    steps += [(d * 3 + 8, diagonal, d) for d in range(nz)]
+    for _, step, d in sorted(steps, key=lambda e: e[0]):
+        waiting = len(late)
+        step(d)
+        drain(waiting)
+    drain(len(late))
+    acc = mix[...]
 
     cosine = cos_ref[pl.ds(pl.multiple_of(x * toks, toks), toks), :]
     sine = sin_ref[pl.ds(pl.multiple_of(x * toks, toks), toks), :]
@@ -490,18 +535,26 @@
         to_core(k).wait_recv()
         return tbuf[k * CORES + c].astype(jnp.float32) + rs1[k].astype(jnp.float32)
 
-    for yy in (1 - y, y):
-        for d, zz in order:
-            term(zz * SIDE + yy, 1 - c)
-            to_core(zz * SIDE + yy).start()
-            term(zz * SIDE + yy, c)
-            if yy is not y:
-                pass
-        if yy is not y:
-            for d, zz in order:
-                ybuf[zz] = core_sum(zz * SIDE + yy).astype(jnp.bfloat16)
-                to_y(zz).start()
-    kept = None
+    def to_y_side(zz):
+        ybuf[zz] = core_sum(zz * SIDE + 1 - y).astype(jnp.bfloat16)
+        to_y(zz).start()
+
+    last = None
+    for d, zz in order:
+        k = zz * SIDE + 1 - y
+        term(k, 1 - c)
+        to_core(k).start()
+        term(k, c)
+        if last is not None:
+            to_y_side(last)
+        last = zz
+    for n, (d, zz) in enumerate(order):
+        k = zz * SIDE + y
+        term(k, 1 - c)
+        to_core(k).start()
+        if n == 0:
+            to_y_side(last)
+        term(k, c)
     for n, (d, zz) in enumerate(order):
         grad_rows(marks[n + 1], marks[n + 2])
         part = core_sum(zz * SIDE + y)
@@ -536,6 +589,11 @@
         to_y(zz).wait_send()
     for d in range(1, nz):
         to_z(d).wait_send()
+
+
+def copy_kernel(*refs):
+    for k in range(4):
+        refs[4 + k][...] = refs[k][...]
 
 
 def fused(n_inter, hidden_in, norm_gain, qkv_weight, attn_cotangent):
@@ -584,6 +642,13 @@
             collective_id=0, has_side_effects=True, vmem_limit_bytes=60 * 2**20
         ),
     )(hidden_in[0], norm_gain[None], qkv_weight, attn_cotangent[0], cosine, sine)
+    outs = (attn, gin, wg, gg)
+    attn, gin, wg, gg = pl.pallas_call(
+        copy_kernel,
+        out_shape=tuple(jax.ShapeDtypeStruct(o.shape, o.dtype) for o in outs),
+        in_specs=[vmem] * 4,
+        out_specs=(vmem,) * 4,
+    )(*outs)
     return attn[None], gin[None], wg, gg[0]
 
 

time: 106 us -> 98.7 us (0.931); the launches traced: 105 us -> 98.5 us
  local copies, waits for them, and re-layouts: 5.17 us -> 0 us
    unnamed x8 -> x0, local copies, waits for them, and re-layouts: 5.17 us -> none
    pallas_call x1, Pallas kernels: 98.9 us -> 95.3 us  [fused(): pl.pallas_call(functools.partial(fused_kernel, n_inter), out_shape=(jax.S...]
    pallas_call x0 -> x1, Pallas kernels: none -> 2.56 us  [fused(): pl.pallas_call(copy_kernel, out_shape=tuple((jax.ShapeDtypeStruct(o.shape...]
where the time goes in v2:
time: 98.7 us; the launch traced here: 98.5 us
  Pallas kernels  97.9 us (99%)
    pallas_call x1, Pallas kernels, fused(): pl.pallas_call(functools.partial(fused_kernel, n_inter), out_shape=(jax.S...  95.3 us
    pallas_call x1, Pallas kernels, fused(): pl.pallas_call(copy_kernel, out_shape=tuple((jax.ShapeDtypeStruct(o.shape...  2.56 us

profile of v2, /device:TPU:0, one launch (start us, length us, event | category | flops | bytes accessed | tf_op | source)
XLA Modules:
  0.0 98.5 jit_solution(10305437212403609842)
XLA Ops:
  0.6 95.3 %shard_map.93 = (bf16[128,512]{1,0:T(8,128)(2,1)}, bf16[128,4096]{1,0:T(8,128)(2,1)}, f32[128,768]{1,0:T(8,128)}, f32[1,128]{1,0:T(1,128)}) custom-call(bf16[128,4096]{1,0:T(8,128)(2,1)} %bitcast.6, bf16[1,128]{1,0:T(2,128)(2,1)} %bitcast.8, bf16[128,768]{1,0:T(8,128)(2,1)} %w_ref.1, bf16[128,512]{1,0:T(8,128)(2,1)} %bitcast.7, ...), custom_call_target="tpu_custom_call" | custom-call | tf_op jit(solution)/shard_map/pallas_call | solution.py:610
  95.9 2.6 %shard_map.94 = (bf16[128,512]{1,0:T(8,128)(2,1)}, bf16[128,4096]{1,0:T(8,128)(2,1)}, f32[128,768]{1,0:T(8,128)}, f32[1,128]{1,0:T(1,128)}) custom-call(bf16[128,512]{1,0:T(8,128)(2,1)} %get-tuple-element.12.refs_0_, bf16[128,4096]{1,0:T(8,128)(2,1)} %get-tuple-element.13.refs_1_, f32[128,768]{1,0:T(8,128)} %get-tuple-element.14.refs_2_, ...), custom_call_target="tpu_custom_call" | custom-call | tf_op jit(solution)/shard_map/pallas_call | solution.py:646

commit v3 on v2

--- a/solution.py
+++ b/solution.py
@@ -251,7 +251,7 @@
     n_inter,
     hid_ref, gain_ref, w_ref, ct_ref, cos_ref, sin_ref,
     attn_ref, gin_ref, wg_ref, gg_ref,
-    wbuf, nrm, nbuf, kvbuf, gkv, gkv_in, gmbuf, tbuf, rs1, ybuf, rs2, zbuf, rs3, mix,
+    wbuf, nrm, nbuf, kvbuf, gkv, gkv_out, gkv_in, gmbuf, tbuf, rs1, ybuf, rs2, zbuf, rs3, mix,
     ag_send, ag_recv, ex_send, ex_recv, c_send, c_recv, y_send, y_recv, z_send, z_recv,
 ):
     i = lax.axis_index("inter")
@@ -445,8 +445,15 @@
     kv_copy = exchange(0, kvbuf.at[here], kvbuf.at[here])
     kv_copy.start()
     keep = pl.ds(pl.multiple_of(x * half, half), half)
-    give = pl.ds(pl.multiple_of((1 - x) * half, half), half)
-    norm_copy = exchange(1, nrm.at[:, give], nbuf.at[here])
+    part = half // 2
+    norm_copy, norm_rest = [
+        exchange(
+            k,
+            nrm.at[:, pl.ds(pl.multiple_of((1 - x) * half + first, part), part)],
+            nbuf.at[here, first : first + part],
+        )
+        for k, first in ((1, 0), (4, part))
+    ]
     norm_copy.start()
     nbuf[here, :] = nrm[:, keep]
     kv_copy.wait()
@@ -470,15 +477,17 @@
     grad_scores = (probs * (nt_dot(grad, values) - delta)).astype(jnp.bfloat16)
     gkv[:, :HD] = tn_dot(grad_scores, query)
     gkv[:, HD:] = tn_dot(probs.astype(jnp.bfloat16), grad)
-    gkv_copy = exchange(2, gkv.at[there], gkv_in)
+    gkv_out[...] = gkv[there, :].astype(jnp.bfloat16)
+    gkv_copy = exchange(2, gkv_out, gkv_in)
     gkv_copy.start()
+    norm_rest.start()
     grad_query = nn_dot(grad_scores, keys)
     for h in range(HEADS):
         gmbuf[here, h * HD : (h + 1) * HD] = (
             unrope(grad_query[h * toks : (h + 1) * toks]) * scale
         ).astype(jnp.bfloat16)
     gkv_copy.wait()
-    own_kv = gkv[here, :] + gkv_in[...]
+    own_kv = gkv[here, :] + gkv_in[...].astype(jnp.float32)
     gmbuf[here, qcols : qcols + HD] = unrope(own_kv[:, :HD]).astype(jnp.bfloat16)
     gmbuf[here, qcols + HD :] = own_kv[:, HD:].astype(jnp.bfloat16)
     gm_copy = exchange(3, gmbuf.at[here], gmbuf.at[here])
@@ -501,6 +510,7 @@
     marks = [2 * n_inter * k // pieces for k in range(pieces + 1)]
     grad_rows(marks[0], marks[1])
     norm_copy.wait()
+    norm_rest.wait()
     gm_copy.wait()
 
     both_gm = gmbuf[...]
@@ -623,7 +633,8 @@
             pltpu.VMEM((2 * toks, width // 2), bf),
             pltpu.VMEM((2 * toks, 2 * HD), bf),
             pltpu.VMEM((2 * toks, 2 * HD), f32),
-            pltpu.VMEM((toks, 2 * HD), f32),
+            pltpu.VMEM((toks, 2 * HD), bf),
+            pltpu.VMEM((toks, 2 * HD), bf),
             pltpu.VMEM((2 * toks, cols), bf),
             pltpu.VMEM((n_inter, rows, cols), bf),
             pltpu.VMEM((chips, rows, cols), bf),
@@ -633,7 +644,7 @@
             pltpu.VMEM((max(nz - 1, 1), rows, cols), bf),
             pltpu.VMEM((toks, cols), f32),
             dma((5, 2 * n_inter)), dma((2 * n_inter,)),
-            dma((4,)), dma((4,)),
+            dma((5,)), dma((5,)),
             dma((chips,)), dma((chips,)),
             dma((nz,)), dma((nz,)),
             dma((max(nz - 1, 1),)), dma((max(nz - 1, 1),)),

time: 98.7 us -> 95 us (0.963)
  Pallas kernels: 97.9 us -> 94.2 us
    pallas_call x1, Pallas kernels: 95.3 us -> 91.6 us  [fused(): pl.pallas_call(functools.partial(fused_kernel, n_inter), out_shape=(jax.S...]
where the time goes in v3:
time: 95 us; the launch traced here: 94.8 us
  Pallas kernels  94.2 us (99%)
    pallas_call x1, Pallas kernels, fused(): pl.pallas_call(functools.partial(fused_kernel, n_inter), out_shape=(jax.S...  91.6 us
    pallas_call x1, Pallas kernels, fused(): pl.pallas_call(copy_kernel, out_shape=tuple((jax.ShapeDtypeStruct(o.shape...  2.56 us

profile of v3, /device:TPU:0, one launch (start us, length us, event | category | flops | bytes accessed | tf_op | source)
XLA Modules:
  0.0 94.8 jit_solution(1826685146638456921)
XLA Ops:
  0.6 91.6 %shard_map.93 = (bf16[128,512]{1,0:T(8,128)(2,1)}, bf16[128,4096]{1,0:T(8,128)(2,1)}, f32[128,768]{1,0:T(8,128)}, f32[1,128]{1,0:T(1,128)}) custom-call(bf16[128,4096]{1,0:T(8,128)(2,1)} %bitcast.6, bf16[1,128]{1,0:T(2,128)(2,1)} %bitcast.8, bf16[128,768]{1,0:T(8,128)(2,1)} %w_ref.1, bf16[128,512]{1,0:T(8,128)(2,1)} %bitcast.7, ...), custom_call_target="tpu_custom_call" | custom-call | tf_op jit(solution)/shard_map/pallas_call | solution.py:620
  92.2 2.6 %shard_map.94 = (bf16[128,512]{1,0:T(8,128)(2,1)}, bf16[128,4096]{1,0:T(8,128)(2,1)}, f32[128,768]{1,0:T(8,128)}, f32[1,128]{1,0:T(1,128)}) custom-call(bf16[128,512]{1,0:T(8,128)(2,1)} %get-tuple-element.12.refs_0_, bf16[128,4096]{1,0:T(8,128)(2,1)} %get-tuple-element.13.refs_1_, f32[128,768]{1,0:T(8,128)} %get-tuple-element.14.refs_2_, ...), custom_call_target="tpu_custom_call" | custom-call | tf_op jit(solution)/shard_map/pallas_call | solution.py:657
